TPU v7x, 32 devices: a whole 2x2x4 slice. The times are simulated.
32 devices in a mesh: lon: 4 (over y, x), lat: 8 (over z, core).
Axes of the slice: x: 2, y: 2, z: 4, core: 2. Of those that a mesh axis runs over, the one named last changes fastest.
Arguments:
- spectrum: float32 [32, 512, 648], P('lon', 'lat'), may hold values from 0.01 to 1
- sea_mask: int32 [32, 512], P('lon', 'lat'), may hold values from 0 to 1, as said below
- ice_flags: int32 [32, 512], P('lon', 'lat'), may hold values 0 or 1
- wind_forcing: float32 [32, 512], P('lon', 'lat'), may hold values from 0.1 to 1.5
- group_speed: float32 [18], replicated, may hold values from 0.3 to 1
- coupling: bfloat16 [648, 648], replicated, may hold values from -0.25 to 0.25
Outputs:
- field: float32 [32, 512, 648], P('lon', 'lat')
Inputs may be any that keep to these rules, and one draw needn't show every extreme that they name: `sea_mask`: each device's block of 8 x 64 cells holds at most 384 sea cells and at least 128; in every draw some block holds exactly 384.
All inputs are finite; a program needn't handle non-finite values. No bound on the sum of `ice_flags` on one device may be relied on, other than what follows from the above.
Results may differ from a plain program's by a relative error of at most 0.00079.
Values sent between devices are 32-bit elements; how exact they have to be, the bound alone decides.
A program may use at most 64 MiB of HBM per device.

v0:
```python
import functools
import math

import jax
import jax.numpy as jnp
from jax import lax
from jax.experimental import pallas as pl
from jax.experimental.pallas import tpu as pltpu
from jax.sharding import PartitionSpec as P

DIRS = 36
STEPS = 4
LANES = 128
PAD = 8
CHUNKS = 4
MESH = pl.DeviceIdType.MESH

time_step = 0.2
dissipation = 0.5


def kernel(
    freqs, speed_hbm, sea_hbm, ice_hbm, wind_hbm, spectrum_ref, coupling_ref, out_ref,
    speed_ref, sea_ref, ice_ref, wind_ref,
    field, staged, weights, east_weights, raw_weights, rounded, kept, keep_x, push_x, push_y, grow, scale,
    east_out, east_in, west_out, west_in, north_out, north_in, south_out, south_in,
    load_sem, small_sem, weight_sem, lon_send, lon_recv, lat_send, lat_recv,
):
    columns, rows, bins = staged.shape
    tiles = field.shape[2]
    piece = rows // CHUNKS
    side_rows = piece // 2
    middle = (CHUNKS - 1) * piece
    ends_chunk = CHUNKS - 1
    middle_at = columns * piece
    mean_of = 1.0 / bins
    quarter, half, late = DIRS // 4 * freqs, DIRS // 2 * freqs, DIRS * 3 // 4 * freqs
    cut_w, cut_y, cut_e = quarter - LANES, half - 2 * LANES, late - 3 * LANES
    late_w = LANES - cut_e
    inside = 64 - late_w - cut_w
    tail = bins - (tiles - 1) * LANES

    lon, lat = lax.axis_index("lon"), lax.axis_index("lat")
    lons, lats = lax.axis_size("lon"), lax.axis_size("lat")
    east, west = lax.rem(lon + 1, lons), lax.rem(lon + lons - 1, lons)
    has_south, has_north = lat > 0, lat < lats - 1
    odd = lax.rem(lon, 2) == 1

    def width(t):
        return LANES if t < tiles - 1 else tail

    last = columns - 1
    edges, inner = [0, last], list(range(1, last))
    loads = [
        pltpu.make_async_copy(spectrum_ref.at[c], staged.at[c], load_sem.at[c])
        for c in range(columns)
    ]
    weight_load = pltpu.make_async_copy(coupling_ref, raw_weights, weight_sem)
    small = [
        pltpu.make_async_copy(source, target, small_sem.at[n])
        for n, (source, target) in enumerate(
            ((sea_hbm, sea_ref), (speed_hbm, speed_ref), (ice_hbm, ice_ref), (wind_hbm, wind_ref))
        )
    ]
    for copy in small:
        copy.start()
    for c in edges:
        loads[c].start()

    barrier = pltpu.get_barrier_semaphore()
    pl.semaphore_signal(barrier, inc=1, device_id=(east, lat), device_id_type=MESH)
    pl.semaphore_signal(barrier, inc=1, device_id=(west, lat), device_id_type=MESH)

    @pl.when(has_south)
    def _():
        pl.semaphore_signal(barrier, inc=1, device_id=(lon, lat - 1), device_id_type=MESH)

    @pl.when(has_north)
    def _():
        pl.semaphore_signal(barrier, inc=1, device_id=(lon, lat + 1), device_id_type=MESH)

    small[0].wait()
    sea = sea_ref[...].astype(jnp.float32)
    sea_rows = jnp.transpose(sea)
    for c in range(columns):
        scale[c] = jnp.broadcast_to(sea_rows[:, c : c + 1], (rows, LANES))

    lane = lax.broadcasted_iota(jnp.int32, (8, LANES), 1)
    lane_piece = lax.broadcasted_iota(jnp.int32, (piece, LANES), 1)
    lane_eight = lax.broadcasted_iota(jnp.int32, (8, LANES), 1)
    row_eight = lax.broadcasted_iota(jnp.int32, (8, LANES), 0)
    own_low = lane_eight // 4 == row_eight + 1
    own_high = lane_eight // 4 == row_eight + 9
    low_half = lane_eight < LANES // 2

    def turn(value, by):
        return pltpu.roll(value, by % LANES, 1)

    def gather_rest(upper, lower, start):
        base = (4 - start) % LANES
        up = pltpu.roll(upper, base, 1, stride=4, stride_axis=0)
        down = pltpu.roll(lower, base + 32, 1, stride=4, stride_axis=0)
        spread = jnp.where(own_low, up, 0.0) + jnp.where(own_high, down, 0.0)
        return jnp.sum(spread, axis=0, keepdims=True)

    def spread_rest(line, start):
        line = jnp.broadcast_to(line, (8, LANES))
        halves = []
        for part in range(2):
            value = turn(line, start - 4 - 32 * part)
            for i in range(1, 8):
                value = jnp.where(row_eight == i, turn(line, start - 4 - 4 * i - 32 * part), value)
            halves.append(value)
        return halves

    def lon_copy(step, side, k):
        out_buf, in_buf, to = ((east_out, west_in, east), (west_out, east_in, west))[side]
        return pltpu.make_async_remote_copy(
            src_ref=out_buf.at[step, k],
            dst_ref=in_buf.at[step, k],
            send_sem=lon_send.at[step, side, k],
            recv_sem=lon_recv.at[step, side, k],
            device_id=(to, lat),
            device_id_type=MESH,
        )

    def lat_copy(step, side):
        out_buf, in_buf, to = ((north_out, south_in, lat + 1), (south_out, north_in, lat - 1))[side]
        return pltpu.make_async_remote_copy(
            src_ref=out_buf.at[step],
            dst_ref=in_buf.at[step],
            send_sem=lat_send.at[step, side],
            recv_sem=lat_recv.at[step, side],
            device_id=(lon, to),
            device_id_type=MESH,
        )

    MIDDLE = [(side_rows, middle)]
    ENDS = [(0, side_rows), (rows - side_rows, side_rows)]

    def spans_of(k):
        return ENDS if k == ends_chunk else [(side_rows + k * piece, piece)]

    def join(parts):
        return parts[0] if len(parts) == 1 else jnp.concatenate(parts, axis=0)

    def read(b, c, t, spans, shift=0):
        return join([field[b, c, t, PAD + at + shift : PAD + at + shift + n, :] for at, n in spans])

    def write(b, c, t, spans, value):
        done = 0
        for at, n in spans:
            field[b, c, t, PAD + at : PAD + at + n, :] = value[done : done + n]
            done += n

    def table(ref, i, spans):
        return join([ref[i, at : at + n, :] for at, n in spans])

    def rounded_at(c, k):
        return c * piece if k == ends_chunk else middle_at + c * middle + k * piece

    def mixed(lane_of, first, fifth, third):
        fifths = jnp.where(lane_of < cut_w + inside, turn(fifth, cut_w), turn(fifth, 64))
        return jnp.where(lane_of < cut_w, first, jnp.where(lane_of < cut_e, fifths, third))

    def pack_east(step, k, zero, four, rest):
        buffer = east_out.at[step, k]
        buffer[0:16, :] = zero
        buffer[16:32, :] = four
        low, high = rest[0:8], rest[8:16]
        buffer[32:40, :] = jnp.where(low_half, turn(low, late_w), turn(high, late_w + 64))
        buffer[40:41, :] = gather_rest(low, high, 64 + inside)

    def pack_west(step, k, one, two, three):
        buffer = west_out.at[step, k]
        buffer[0:16, :] = two
        buffer[16:32, :] = jnp.where(lane_piece < cut_e, three, one)
        low, high = one[0:8], one[8:16]
        buffer[32:40, :] = jnp.where(low_half, turn(low, -cut_w), turn(high, 64 - cut_w))
        buffer[40:41, :] = gather_rest(low, high, 64 + cut_w)

    def send_north(step):
        b = step % 2
        edge = slice(PAD + rows - 1, PAD + rows)
        for c in range(columns):
            for i in range(3):
                north_out[step, i, c : c + 1, :] = field[b, c, i, edge, :]

        @pl.when(has_north)
        def _():
            lat_copy(step, 0).start()

    def send_south(step):
        b = step % 2
        low = lane[0:1] < cut_y
        edge = slice(PAD, PAD + 1)
        for c in range(columns):
            south_out[step, 0, c : c + 1, :] = jnp.where(
                low, field[b, c, 5, edge, :], field[b, c, 2, edge, :]
            )
            for i in range(1, 3):
                south_out[step, i, c : c + 1, :] = field[b, c, i + 2, edge, :]

        @pl.when(has_south)
        def _():
            lat_copy(step, 1).start()

    def take_south(step):
        b = step % 2

        @pl.when(has_south)
        def _():
            lat_copy(step, 0).wait_recv()
            for c in range(columns):
                for i in range(3):
                    field[b, c, i, PAD - 1 : PAD, :] = south_in[step, i, c : c + 1, :]

    def take_north(step):
        b = step % 2
        edge = slice(PAD + rows, PAD + rows + 1)

        @pl.when(has_north)
        def _():
            lat_copy(step, 1).wait_recv()
            for c in range(columns):
                for i, t in ((0, 2), (1, 3), (2, 4), (0, 5)):
                    field[b, c, t, edge, :] = north_in[step, i, c : c + 1, :]

    def west_halo(step, k):
        buffer = west_in.at[step, k]
        main = buffer[32:40, :]
        rest = spread_rest(buffer[40:41, :], inside)
        shared = jnp.concatenate([turn(main, -late_w), turn(main, 64 - late_w)], axis=0)
        ends = [
            jnp.where(lane_eight < inside, turn(main, 64 * part + inside - 64), rest[part])
            for part in range(2)
        ]
        return {
            0: buffer[0:16, :],
            1: shared,
            3: shared,
            4: buffer[16:32, :],
            5: jnp.concatenate(ends, axis=0),
        }

    def east_halo(step, k):
        buffer = east_in.at[step, k]
        main, shared = buffer[32:40, :], buffer[16:32, :]
        rest = spread_rest(buffer[40:41, :], 64 + cut_w)
        moved = [
            jnp.where(lane_eight < 64 + cut_w, turn(main, cut_w - 64 * part), rest[part])
            for part in range(2)
        ]
        moved = jnp.concatenate(moved, axis=0)
        return {1: jnp.where(lane_piece < cut_e, moved, shared), 2: buffer[0:16, :], 3: shared}

    def advect(b, c, t, spans, from_west, from_east):
        lanes = lax.broadcasted_iota(jnp.int32, (sum(n for _, n in spans), LANES), 1)
        if t == 1:
            beside = jnp.where(lanes < cut_w, from_west(t), from_east(t))
        elif t == 2:
            beside = from_east(t)
        elif t == 3:
            beside = jnp.where(lanes < cut_e, from_east(t), from_west(t))
        else:
            beside = from_west(t)
        if t < 2:
            along = read(b, c, t, spans, -1)
        elif t == 2:
            along = jnp.where(lanes < cut_y, read(b, c, t, spans, -1), read(b, c, t, spans, 1))
        else:
            along = read(b, c, t, spans, 1)
        return (
            table(keep_x, t, spans) * read(b, c, t, spans)
            + table(push_x, t, spans) * beside
            + push_y[t, 0:1, :] * along
        )

    def advect_cell(step, c, spans, row, from_west, from_east):
        b = step % 2
        values, total = [], None
        n = sum(count for _, count in spans)
        for t in range(tiles):
            value = advect(b, c, t, spans, from_west, from_east)
            values.append(value)
            rounded[row : row + n, t * LANES : (t + 1) * LANES] = value.astype(jnp.bfloat16)
            total = value if total is None else total + value
        energy = jnp.sum(total, axis=1, keepdims=True) * mean_of
        growth = table(grow, c, spans) - (time_step * dissipation) * energy * table(scale, c, spans)
        return values, growth

    def advect_edge(step, side, k, row):
        b, spans = step % 2, spans_of(k)
        if side == 0:
            c, halo = 0, west_halo(step, k)
            return advect_cell(
                step, c, spans, row, lambda t: halo[t], lambda t: read(b, 1, t, spans)
            )
        c, halo = last, east_halo(step, k)
        return advect_cell(
            step, c, spans, row, lambda t: read(b, last - 1, t, spans), lambda t: halo[t]
        )

    def keep(c, spans, value):
        done = 0
        for at, n in spans:
            kept[c, at : at + n, :] = value[done : done + n]
            done += n

    def prepare(step, ends, group):
        b, spans = step % 2, ENDS if ends else MIDDLE
        deep = piece if ends else middle
        start = 0 if ends else middle_at
        for c in group:
            values, growth = advect_cell(
                step, c, spans, start + c * deep,
                lambda t, c=c: read(b, c - 1, t, spans), lambda t, c=c: read(b, c + 1, t, spans),
            )
            keep(c, spans, growth)
            for t in range(tiles):
                write(1 - b, c, t, spans, values[t])

    def edge(step, messages, filler=None):
        b = step % 2
        for side, k in messages:
            lon_copy(step, side, k).wait_recv()
        with jax.named_scope(f"edge#s={step}#k={messages[0][1]}#d={messages[0][0]}"):
            advected = []
            for side, k in messages:
                c, spans = 0 if side == 0 else last, spans_of(k)
                values, growth = advect_edge(step, side, k, rounded_at(c, k))
                keep(c, spans, growth)
                for t in range(tiles):
                    if t not in ((1, 2, 3), (0, 4))[side]:
                        write(1 - b, c, t, spans, values[t])
                if side == 1:
                    values[1] = mixed(lane_piece, values[1], values[5], values[3])
                advected.append((values, growth))
            products = []
            for side, k in messages:
                row = rounded_at(0 if side == 0 else last, k)
                part = weights[:, LANES : 4 * LANES] if side == 0 else east_weights[...]
                products.append(
                    jnp.dot(rounded[row : row + piece, :], part, preferred_element_type=jnp.float32)
                )
            if filler is not None:
                filler()
            for (side, k), (values, growth), transfer in zip(messages, advected, products):
                c, spans = 0 if side == 0 else last, spans_of(k)
                sea_here = time_step * table(scale, c, spans)
                sent = ((1, 2, 3), (0, 4, 1))[side]
                new = [
                    growth * values[t] + sea_here * transfer[:, i * LANES : (i + 1) * LANES]
                    for i, t in enumerate(sent)
                ]
                (pack_west, pack_east)[side](step + 1, k, *new)
                for t, value in list(zip(sent, new))[: 3 - side]:
                    write(1 - b, c, t, spans, value)
                lon_copy(step + 1, 1 - side, k).start()

    def block(step, ends):
        with jax.named_scope(f"block#s={step}#e={int(ends)}"):
            b, final = step % 2, step == STEPS - 1
            spans = ENDS if ends else MIDDLE
            deep = piece if ends else middle
            start = 0 if ends else middle_at
            first, count = (1, columns - 2) if final else (0, columns)
            transfer = jnp.dot(
                rounded[start + first * deep : start + (first + count) * deep, :], weights[...],
                preferred_element_type=jnp.float32,
            )
            for c in inner if final else range(columns):
                sea_here = time_step * table(scale, c, spans)
                growth = table(kept, c, spans)
                row = (c - first) * deep
                for t in (0, 4, 5) if c == 0 else (1, 2, 3, 5) if c == last else range(tiles):
                    moved = transfer[row : row + deep, t * LANES : (t + 1) * LANES]
                    value = growth * read(1 - b, c, t, spans) + sea_here * moved
                    if final:
                        emit(c, t, spans, value)
                    else:
                        write(1 - b, c, t, spans, value)

    def emit(c, t, spans, value):
        w, done = width(t), 0
        for at, n in spans:
            out_ref[c, at : at + n, t * LANES : t * LANES + w] = value[done : done + n, 0:w]
            done += n

    def finish(step, chunks):
        for side, k in chunks:
            lon_copy(step, side, k).wait_recv()
        with jax.named_scope(f"finish#n={len(chunks)}"):
            done = []
            for n, (side, k) in enumerate(chunks):
                done.append(advect_edge(step, side, k, n * piece))
            transfer = jnp.dot(
                rounded[0 : len(chunks) * piece, :], weights[...], preferred_element_type=jnp.float32
            )
            for n, (side, k) in enumerate(chunks):
                values, growth = done[n]
                c, spans = 0 if side == 0 else last, spans_of(k)
                sea_here = time_step * table(scale, c, spans)
                for t in range(tiles):
                    moved = transfer[n * piece : (n + 1) * piece, t * LANES : (t + 1) * LANES]
                    emit(c, t, spans, growth * values[t] + sea_here * moved)

    def by_side(step_of):
        @pl.when(odd)
        def _():
            step_of(1, 0)

        @pl.when(jnp.logical_not(odd))
        def _():
            step_of(0, 1)

    def take_column(c):
        for t in range(tiles):
            w = width(t)
            field[0, c, t, PAD : PAD + rows, 0:w] = (
                staged[c, :, t * LANES : t * LANES + w] * scale[c, :, 0:w]
            )

    for c in edges:
        field[0, c, tiles - 1, PAD : PAD + rows, :] = jnp.zeros((rows, LANES), jnp.float32)
    for c in edges:
        loads[c].wait()
    for c in inner:
        loads[c].start()
    weight_load.start()
    for c in edges:
        take_column(c)
    for k in range(CHUNKS):
        spans = spans_of(k)
        pack_west(0, k, *(read(0, 0, t, spans) for t in (1, 2, 3)))
        mine = [read(0, last, t, spans) for t in range(tiles)]
        pack_east(0, k, mine[0], mine[4], mixed(lane_piece, mine[1], mine[5], mine[3]))

    with jax.named_scope("barrier"):
        heard = 2 + has_south.astype(jnp.int32) + has_north.astype(jnp.int32)
        pl.semaphore_wait(barrier, heard)

    def send_first(first, second):
        for k in range(CHUNKS):
            lon_copy(0, 1 - first, k).start()
        for k in [ends_chunk] + list(range(CHUNKS - 1)):
            lon_copy(0, 1 - second, k).start()

    by_side(send_first)

    for copy in small[1:]:
        copy.wait()
    forcing = wind_ref[...] * (1.0 - ice_ref[...].astype(jnp.float32))
    growth = jnp.transpose(sea * (1.0 + time_step * forcing))
    for c in range(columns):
        grow[c] = jnp.broadcast_to(growth[:, c : c + 1], (rows, LANES))
    row = lax.broadcasted_iota(jnp.int32, (rows, LANES), 0) + lat * rows
    latitude = (-60.0 + 120.0 * (row.astype(jnp.float32) + 0.5) / (rows * lats)) * (math.pi / 180.0)
    inverse = 1.0 / jnp.cos(latitude)
    for t in range(tiles):
        number = (lane + t * LANES).astype(jnp.float32)
        direction = jnp.floor((number + 0.5) * (1.0 / freqs))
        freq = number - direction * freqs
        speed = jnp.zeros((8, LANES), jnp.float32)
        for f in range(freqs):
            speed = jnp.where(freq == f, speed_ref[f], speed)
        real = (lane + t * LANES) < bins
        theta = (direction + 0.5) * (2.0 * math.pi / DIRS)
        along_y = jnp.where(real, jnp.abs(0.45 * jnp.sin(theta) * speed), 0.0)
        along_x = jnp.where(real, jnp.abs(0.225 * jnp.cos(theta) * speed), 0.0)
        push_y[t] = along_y
        along_x = along_x[0:1] * inverse
        push_x[t] = along_x
        keep_x[t] = 1.0 - along_x - along_y[0:1]

    zero_row = jnp.zeros((1, LANES), jnp.float32)
    for c in range(columns):
        for t in range(tiles):
            for b in range(2):
                field[b, c, t, PAD - 1 : PAD, :] = zero_row
                field[b, c, t, PAD + rows : PAD + rows + 1, :] = zero_row
        if c in inner:
            field[0, c, tiles - 1, PAD : PAD + rows, :] = jnp.zeros((rows, LANES), jnp.float32)

    for c in inner:
        loads[c].wait()
        take_column(c)
    send_north(0)
    send_south(0)

    weight_load.wait()
    weights[...] = jnp.zeros_like(weights)
    weights[0:bins, 0:bins] = raw_weights[...]
    wide_lane = lax.broadcasted_iota(jnp.int32, (tiles * LANES, LANES), 1)
    east_weights[:, 0:LANES] = weights[:, 0:LANES]
    east_weights[:, LANES : 2 * LANES] = weights[:, 4 * LANES : 5 * LANES]
    first, third, fifth = (
        weights[:, t * LANES : (t + 1) * LANES].astype(jnp.float32) for t in (1, 3, 5)
    )
    east_weights[:, 2 * LANES : 3 * LANES] = mixed(wide_lane, first, fifth, third).astype(jnp.bfloat16)

    share = -(-len(inner) // (CHUNKS - 1))
    for step in range(STEPS):
        if step < STEPS - 1:

            def before(first, second):
                for k in range(CHUNKS - 1):
                    group = inner[k * share : (k + 1) * share]
                    edge(step, [(first, k)], lambda: prepare(step, False, group))
                take_south(step)
                take_north(step)
                edge(
                    step, [(first, ends_chunk), (second, ends_chunk)],
                    lambda: prepare(step, True, inner),
                )

            def after(first, second):
                for k in range(CHUNKS - 1):
                    edge(step, [(second, k)])

            by_side(before)
            block(step, True)
            send_south(step + 1)
            send_north(step + 1)
            by_side(after)
            block(step, False)
        else:
            prepare(step, False, inner)
            block(step, False)
            take_south(step)
            take_north(step)
            prepare(step, True, inner)
            block(step, True)

            def close(first, second):
                finish(step, [(first, k) for k in range(CHUNKS - 1)])
                finish(step, [(first, ends_chunk)] + [(second, k) for k in range(CHUNKS)])

            by_side(close)
    for step in range(STEPS):
        for k in range(CHUNKS):
            for side in range(2):
                lon_copy(step, side, k).wait_send()

        @pl.when(has_north)
        def _():
            lat_copy(step, 0).wait_send()

        @pl.when(has_south)
        def _():
            lat_copy(step, 1).wait_send()


def on_device(spectrum, sea_mask, ice_flags, wind_forcing, group_speed, coupling):
    columns, rows, bins = spectrum.shape
    tiles = -(-bins // LANES)
    wide = tiles * LANES
    piece = rows // CHUNKS
    hbm = pl.BlockSpec(memory_space=pltpu.HBM)
    operands = (group_speed, sea_mask, ice_flags, wind_forcing, spectrum, coupling)
    f32 = jnp.float32
    lon_buffer = pltpu.VMEM((STEPS, CHUNKS, 41, LANES), f32)
    lat_buffer = pltpu.VMEM((STEPS, 3, columns, LANES), f32)
    return pl.pallas_call(
        functools.partial(kernel, group_speed.shape[0]),
        out_shape=jax.ShapeDtypeStruct(spectrum.shape, spectrum.dtype),
        in_specs=[hbm] * 6,
        out_specs=pl.BlockSpec(memory_space=pltpu.VMEM),
        scratch_shapes=[
            pltpu.SMEM(group_speed.shape, f32),
            pltpu.VMEM((columns, rows), jnp.int32),
            pltpu.VMEM((columns, rows), jnp.int32),
            pltpu.VMEM((columns, rows), f32),
            pltpu.VMEM((2, columns, tiles, rows + 2 * PAD, LANES), f32),
            pltpu.VMEM((columns, rows, bins), f32),
            pltpu.VMEM((wide, wide), jnp.bfloat16),
            pltpu.VMEM((wide, 3 * LANES), jnp.bfloat16),
            pltpu.VMEM((bins, bins), jnp.bfloat16),
            pltpu.VMEM((columns * rows, wide), jnp.bfloat16),
            pltpu.VMEM((columns, rows, LANES), f32),
            pltpu.VMEM((tiles, rows, LANES), f32),
            pltpu.VMEM((tiles, rows, LANES), f32),
            pltpu.VMEM((tiles, 8, LANES), f32),
            pltpu.VMEM((columns, rows, LANES), f32),
            pltpu.VMEM((columns, rows, LANES), f32),
            lon_buffer, lon_buffer, lon_buffer, lon_buffer,
            lat_buffer, lat_buffer, lat_buffer, lat_buffer,
            pltpu.SemaphoreType.DMA((columns,)),
            pltpu.SemaphoreType.DMA((4,)),
            pltpu.SemaphoreType.DMA,
            pltpu.SemaphoreType.DMA((STEPS, 2, CHUNKS)),
            pltpu.SemaphoreType.DMA((STEPS, 2, CHUNKS)),
            pltpu.SemaphoreType.DMA((STEPS, 2)),
            pltpu.SemaphoreType.DMA((STEPS, 2)),
        ],
        compiler_params=pltpu.CompilerParams(
            collective_id=0, has_side_effects=True, vmem_limit_bytes=32 * 1024 * 1024
        ),
    )(*(pltpu.with_memory_space_constraint(x, pltpu.HBM) for x in operands))


def solution(mesh):
    placed = (P("lon", "lat", None), P("lon", "lat"), P("lon", "lat"), P("lon", "lat"), P(), P())
    return jax.shard_map(
        on_device, mesh=mesh, in_specs=placed, out_specs=P("lon", "lat", None), check_vma=False
    )
```

profile of v0, /device:TPU:0, one launch (start us, length us, event | category | flops | bytes accessed | tf_op | source)
XLA Modules:
  0.0 23.5 jit_solution(5214352883400311692)
XLA Ops:
  0.0 22.3 %shard_map.64 = f32[8,64,648]{2,1,0:T(8,128)S(1)} custom-call(f32[18]{0:T(128)} %speed_hbm.1, s32[8,64]{1,0:T(8,128)} %sea_hbm.1, s32[8,64]{1,0:T(8,128)} %ice_hbm.1, f32[8,64]{1,0:T(8,128)} %wind_hbm.1, f32[8,64,648]{2,1,0:T(8,128)} %spectrum_ref.1, bf16[648,648]{1,0:T(8,128)(2,1)} %coupling_ref.1), custom_call_target="tpu_custom_call" | custom-call | tf_op jit(solution)/shard_map/pallas_call | solution.py:564
  22.3 1.1 %copy.8 = f32[8,64,648]{2,1,0:T(8,128)} copy(f32[8,64,648]{2,1,0:T(8,128)S(1)} %shard_map.64) | data formatting | bytes 2654208
where the time goes:
time: 23.7 us; the launch traced here: 23.5 us
  Pallas kernels  22.3 us (94%)
  local copies, waits for them, and re-layouts  1.15 us (5%)
    pallas_call x1, Pallas kernels, on_device(): pl.pallas_call(functools.partial(kernel, group_speed.shape[0]), out_shape...  22.3 us
    unnamed x1, local copies, waits for them, and re-layouts  1.15 us

commit v1 on v0

--- a/solution.py
+++ b/solution.py
@@ -52,9 +52,17 @@
     last = columns - 1
     edges, inner = [0, last], list(range(1, last))
     loads = [
-        pltpu.make_async_copy(spectrum_ref.at[c], staged.at[c], load_sem.at[c])
+        pltpu.make_async_copy(
+            spectrum_ref.at[c], staged.at[c], load_sem.at[0 if c in edges else 1]
+        )
         for c in range(columns)
     ]
+    edge_loads, inner_loads = (
+        pltpu.make_async_copy(
+            spectrum_ref.at[0:count], staged.at[0:count], load_sem.at[n]
+        )
+        for n, count in enumerate((2, columns - 2))
+    )
     weight_load = pltpu.make_async_copy(coupling_ref, raw_weights, weight_sem)
     small = [
         pltpu.make_async_copy(source, target, small_sem.at[n])
@@ -62,22 +70,22 @@
             ((sea_hbm, sea_ref), (speed_hbm, speed_ref), (ice_hbm, ice_ref), (wind_hbm, wind_ref))
         )
     ]
+    barrier = pltpu.get_barrier_semaphore()
+    pl.semaphore_signal(barrier, inc=1, device_id=(east, lat), device_id_type=MESH)
+    pl.semaphore_signal(barrier, inc=1, device_id=(west, lat), device_id_type=MESH)
+
+    @pl.when(has_south)
+    def _():
+        pl.semaphore_signal(barrier, inc=1, device_id=(lon, lat - 1), device_id_type=MESH)
+
+    @pl.when(has_north)
+    def _():
+        pl.semaphore_signal(barrier, inc=1, device_id=(lon, lat + 1), device_id_type=MESH)
+
     for copy in small:
         copy.start()
     for c in edges:
         loads[c].start()
-
-    barrier = pltpu.get_barrier_semaphore()
-    pl.semaphore_signal(barrier, inc=1, device_id=(east, lat), device_id_type=MESH)
-    pl.semaphore_signal(barrier, inc=1, device_id=(west, lat), device_id_type=MESH)
-
-    @pl.when(has_south)
-    def _():
-        pl.semaphore_signal(barrier, inc=1, device_id=(lon, lat - 1), device_id_type=MESH)
-
-    @pl.when(has_north)
-    def _():
-        pl.semaphore_signal(barrier, inc=1, device_id=(lon, lat + 1), device_id_type=MESH)
 
     small[0].wait()
     sea = sea_ref[...].astype(jnp.float32)
@@ -118,8 +126,8 @@
         return pltpu.make_async_remote_copy(
             src_ref=out_buf.at[step, k],
             dst_ref=in_buf.at[step, k],
-            send_sem=lon_send.at[step, side, k],
-            recv_sem=lon_recv.at[step, side, k],
+            send_sem=lon_send.at[side],
+            recv_sem=lon_recv.at[step % 2, side, k],
             device_id=(to, lat),
             device_id_type=MESH,
         )
@@ -129,8 +137,8 @@
         return pltpu.make_async_remote_copy(
             src_ref=out_buf.at[step],
             dst_ref=in_buf.at[step],
-            send_sem=lat_send.at[step, side],
-            recv_sem=lat_recv.at[step, side],
+            send_sem=lat_send.at[side],
+            recv_sem=lat_recv.at[step % 2, side],
             device_id=(lon, to),
             device_id_type=MESH,
         )
@@ -163,7 +171,7 @@
         fifths = jnp.where(lane_of < cut_w + inside, turn(fifth, cut_w), turn(fifth, 64))
         return jnp.where(lane_of < cut_w, first, jnp.where(lane_of < cut_e, fifths, third))
 
-    def pack_east(step, k, zero, four, rest):
+    def pack_east(step, k, rest, zero, four):
         buffer = east_out.at[step, k]
         buffer[0:16, :] = zero
         buffer[16:32, :] = four
@@ -339,22 +347,26 @@
             products = []
             for side, k in messages:
                 row = rounded_at(0 if side == 0 else last, k)
-                part = weights[:, LANES : 4 * LANES] if side == 0 else east_weights[...]
-                products.append(
-                    jnp.dot(rounded[row : row + piece, :], part, preferred_element_type=jnp.float32)
-                )
+                part, at = (weights, LANES) if side == 0 else (east_weights, 0)
+                products.append([
+                    jnp.dot(
+                        rounded[row : row + piece, :], part[:, at + i * LANES : at + (i + 1) * LANES],
+                        preferred_element_type=jnp.float32,
+                    )
+                    for i in range(3)
+                ])
             if filler is not None:
                 filler()
             for (side, k), (values, growth), transfer in zip(messages, advected, products):
                 c, spans = 0 if side == 0 else last, spans_of(k)
                 sea_here = time_step * table(scale, c, spans)
-                sent = ((1, 2, 3), (0, 4, 1))[side]
+                sent = ((1, 2, 3), (1, 0, 4))[side]
                 new = [
-                    growth * values[t] + sea_here * transfer[:, i * LANES : (i + 1) * LANES]
+                    growth * values[t] + sea_here * transfer[i]
                     for i, t in enumerate(sent)
                 ]
                 (pack_west, pack_east)[side](step + 1, k, *new)
-                for t, value in list(zip(sent, new))[: 3 - side]:
+                for t, value in list(zip(sent, new))[side:]:
                     write(1 - b, c, t, spans, value)
                 lon_copy(step + 1, 1 - side, k).start()
 
@@ -423,8 +435,7 @@
 
     for c in edges:
         field[0, c, tiles - 1, PAD : PAD + rows, :] = jnp.zeros((rows, LANES), jnp.float32)
-    for c in edges:
-        loads[c].wait()
+    edge_loads.wait()
     for c in inner:
         loads[c].start()
     weight_load.start()
@@ -434,7 +445,7 @@
         spans = spans_of(k)
         pack_west(0, k, *(read(0, 0, t, spans) for t in (1, 2, 3)))
         mine = [read(0, last, t, spans) for t in range(tiles)]
-        pack_east(0, k, mine[0], mine[4], mixed(lane_piece, mine[1], mine[5], mine[3]))
+        pack_east(0, k, mixed(lane_piece, mine[1], mine[5], mine[3]), mine[0], mine[4])
 
     with jax.named_scope("barrier"):
         heard = 2 + has_south.astype(jnp.int32) + has_north.astype(jnp.int32)
@@ -482,8 +493,8 @@
         if c in inner:
             field[0, c, tiles - 1, PAD : PAD + rows, :] = jnp.zeros((rows, LANES), jnp.float32)
 
+    inner_loads.wait()
     for c in inner:
-        loads[c].wait()
         take_column(c)
     send_north(0)
     send_south(0)
@@ -492,12 +503,12 @@
     weights[...] = jnp.zeros_like(weights)
     weights[0:bins, 0:bins] = raw_weights[...]
     wide_lane = lax.broadcasted_iota(jnp.int32, (tiles * LANES, LANES), 1)
-    east_weights[:, 0:LANES] = weights[:, 0:LANES]
-    east_weights[:, LANES : 2 * LANES] = weights[:, 4 * LANES : 5 * LANES]
+    east_weights[:, LANES : 2 * LANES] = weights[:, 0:LANES]
+    east_weights[:, 2 * LANES : 3 * LANES] = weights[:, 4 * LANES : 5 * LANES]
     first, third, fifth = (
         weights[:, t * LANES : (t + 1) * LANES].astype(jnp.float32) for t in (1, 3, 5)
     )
-    east_weights[:, 2 * LANES : 3 * LANES] = mixed(wide_lane, first, fifth, third).astype(jnp.bfloat16)
+    east_weights[:, 0:LANES] = mixed(wide_lane, first, fifth, third).astype(jnp.bfloat16)
 
     share = -(-len(inner) // (CHUNKS - 1))
     for step in range(STEPS):
@@ -537,18 +548,21 @@
                 finish(step, [(first, ends_chunk)] + [(second, k) for k in range(CHUNKS)])
 
             by_side(close)
-    for step in range(STEPS):
-        for k in range(CHUNKS):
-            for side in range(2):
-                lon_copy(step, side, k).wait_send()
-
-        @pl.when(has_north)
+    for side, (out_buf, in_buf) in enumerate(((east_out, west_in), (west_out, east_in))):
+        pltpu.make_async_remote_copy(
+            src_ref=out_buf, dst_ref=in_buf, send_sem=lon_send.at[side],
+            recv_sem=lon_recv.at[0, side, 0], device_id=(east, lat), device_id_type=MESH,
+        ).wait_send()
+    for side, (out_buf, in_buf, there) in enumerate(
+        ((north_out, south_in, has_north), (south_out, north_in, has_south))
+    ):
+
+        @pl.when(there)
         def _():
-            lat_copy(step, 0).wait_send()
-
-        @pl.when(has_south)
-        def _():
-            lat_copy(step, 1).wait_send()
+            pltpu.make_async_remote_copy(
+                src_ref=out_buf, dst_ref=in_buf, send_sem=lat_send.at[side],
+                recv_sem=lat_recv.at[0, side], device_id=(east, lat), device_id_type=MESH,
+            ).wait_send()
 
 
 def on_device(spectrum, sea_mask, ice_flags, wind_forcing, group_speed, coupling):
@@ -585,13 +599,13 @@
             pltpu.VMEM((columns, rows, LANES), f32),
             lon_buffer, lon_buffer, lon_buffer, lon_buffer,
             lat_buffer, lat_buffer, lat_buffer, lat_buffer,
-            pltpu.SemaphoreType.DMA((columns,)),
+            pltpu.SemaphoreType.DMA((2,)),
             pltpu.SemaphoreType.DMA((4,)),
             pltpu.SemaphoreType.DMA,
-            pltpu.SemaphoreType.DMA((STEPS, 2, CHUNKS)),
-            pltpu.SemaphoreType.DMA((STEPS, 2, CHUNKS)),
-            pltpu.SemaphoreType.DMA((STEPS, 2)),
-            pltpu.SemaphoreType.DMA((STEPS, 2)),
+            pltpu.SemaphoreType.DMA((2,)),
+            pltpu.SemaphoreType.DMA((2, 2, CHUNKS)),
+            pltpu.SemaphoreType.DMA((2,)),
+            pltpu.SemaphoreType.DMA((2, 2)),
         ],
         compiler_params=pltpu.CompilerParams(
             collective_id=0, has_side_effects=True, vmem_limit_bytes=32 * 1024 * 1024

time: 23.7 us -> 23 us (0.970)
  Pallas kernels: 22.3 us -> 21.7 us
    pallas_call x1, Pallas kernels: 22.3 us -> 21.7 us  [on_device(): pl.pallas_call(functools.partial(kernel, group_speed.shape[0]), out_shape...]
where the time goes in v1:
time: 23 us; the launch traced here: 22.9 us
  Pallas kernels  21.7 us (94%)
  local copies, waits for them, and re-layouts  1.15 us (5%)
    pallas_call x1, Pallas kernels, on_device(): pl.pallas_call(functools.partial(kernel, group_speed.shape[0]), out_shape...  21.7 us
    unnamed x1, local copies, waits for them, and re-layouts  1.15 us

profile of v1, /device:TPU:0, one launch (start us, length us, event | category | flops | bytes accessed | tf_op | source)
XLA Modules:
  0.0 22.9 jit_solution(4619849628858950524)
XLA Ops:
  0.0 21.7 %shard_map.64 = f32[8,64,648]{2,1,0:T(8,128)S(1)} custom-call(f32[18]{0:T(128)} %speed_hbm.1, s32[8,64]{1,0:T(8,128)} %sea_hbm.1, s32[8,64]{1,0:T(8,128)} %ice_hbm.1, f32[8,64]{1,0:T(8,128)} %wind_hbm.1, f32[8,64,648]{2,1,0:T(8,128)} %spectrum_ref.1, bf16[648,648]{1,0:T(8,128)(2,1)} %coupling_ref.1), custom_call_target="tpu_custom_call" | custom-call | tf_op jit(solution)/shard_map/pallas_call | solution.py:578
  21.7 1.1 %copy.8 = f32[8,64,648]{2,1,0:T(8,128)} copy(f32[8,64,648]{2,1,0:T(8,128)S(1)} %shard_map.64) | data formatting | bytes 2654208

commit v2 on v1

--- a/solution.py
+++ b/solution.py
@@ -533,6 +533,11 @@
             block(step, True)
             send_south(step + 1)
             send_north(step + 1)
+
+            @pl.when(lax.rem(lat, 2) == 1)
+            def _():
+                pl.delay(700)
+
             by_side(after)
             block(step, False)
         else:

time: 23 us -> 22.9 us (level)
    pallas_call x1, Pallas kernels: 21.7 us -> 21.5 us  [on_device(): pl.pallas_call(functools.partial(kernel, group_speed.shape[0]), out_shape...]
where the time goes in v2:
time: 22.9 us; the launch traced here: 22.6 us
  Pallas kernels  21.5 us (94%)
  local copies, waits for them, and re-layouts  1.15 us (5%)
    pallas_call x1, Pallas kernels, on_device(): pl.pallas_call(functools.partial(kernel, group_speed.shape[0]), out_shape...  21.5 us
    unnamed x1, local copies, waits for them, and re-layouts  1.15 us

profile of v2, /device:TPU:0, one launch (start us, length us, event | category | flops | bytes accessed | tf_op | source)
XLA Modules:
  0.0 22.6 jit_solution(15690691503627196852)
XLA Ops:
  0.0 21.5 %shard_map.64 = f32[8,64,648]{2,1,0:T(8,128)S(1)} custom-call(f32[18]{0:T(128)} %speed_hbm.1, s32[8,64]{1,0:T(8,128)} %sea_hbm.1, s32[8,64]{1,0:T(8,128)} %ice_hbm.1, f32[8,64]{1,0:T(8,128)} %wind_hbm.1, f32[8,64,648]{2,1,0:T(8,128)} %spectrum_ref.1, bf16[648,648]{1,0:T(8,128)(2,1)} %coupling_ref.1), custom_call_target="tpu_custom_call" | custom-call | tf_op jit(solution)/shard_map/pallas_call | solution.py:583
  21.5 1.1 %copy.8 = f32[8,64,648]{2,1,0:T(8,128)} copy(f32[8,64,648]{2,1,0:T(8,128)S(1)} %shard_map.64) | data formatting | bytes 2654208
